TPU v7x, 512 devices: a 8x2x16 block of a 8x8x16 slice. The times are simulated.
512 devices in a mesh: group: 2 (over y), seq: 16 (over z), batch: 8 (over x), head: 2 (over core).
Axes of the slice: x: 8, y: 2, z: 16, core: 2. Of those that a mesh axis runs over, the one named last changes fastest.
The devices are a block of a 8x8x16 slice.
Arguments:
- queries: bfloat16 [32, 4, 128, 576], P(('group', 'batch'), None, ('seq', 'head')), parts along dimension 0, may hold values from -40 to 40
- cache: bfloat16 [32, 32768, 576], P(('group', 'batch'), 'seq'), parts along dimension 0, may hold values from -6 to 6
- lengths: int32 [32], P(('group', 'batch')), parts along dimension 0, may hold values from 5 to 32768, as said below
Outputs:
- attended: bfloat16 [32, 4, 128, 512], P(('group', 'batch'), None, ('seq', 'head')), parts along dimension 0
There are 2 independent parts, one for each index of `group`. A program takes and returns all parts, laid end to end along the dimension named above; each array names one. Nothing has to cross between parts.
Inputs may be any that keep to these rules, and one draw needn't show every extreme that they name: `lengths`: at least one sequence has length exactly 32768.
All inputs are finite; a program needn't handle non-finite values.
Results may differ from a plain program's by a relative error of at most 0.0065.
Values may be sent and summed in bfloat16 or wider, within the bound.
No kernel may reach another device: no remote copies, remote signals or barrier semaphores. Data moves between devices by JAX's collectives and lax.ppermute only.
A program may use at most 64 MiB of HBM per device.

v0:
```python
import jax
import jax.numpy as jnp
from jax import lax
from jax.sharding import PartitionSpec as P

LAT = 512
ROPE = 64
NOPE = 128


def in_order(tiles, dim):
    tiles = jnp.moveaxis(tiles, 0, dim)
    lengths = tiles.shape
    return tiles.reshape(*lengths[:dim], lengths[dim] * lengths[dim + 1], *lengths[dim + 2 :])


def copy_for_each(array, axis):
    copies = jnp.broadcast_to(array, (lax.axis_size(axis), *array.shape))
    return lax.all_to_all(copies, axis, split_axis=0, concat_axis=0, tiled=True)


def collect(array, axis, dim):
    return in_order(copy_for_each(array, axis), dim)


def of_everyone(array, axis):
    everything = copy_for_each(array, axis)
    return jnp.max(everything, axis=0)


def split_up(array, dim, length):
    before, after = (array.shape[:dim], array.shape[dim + 1 :])
    return jnp.moveaxis(array.reshape(*before, length, -1, *after), dim, 0)


def summed_on_arrival(array, axis, dim):
    tiles = split_up(array, dim, lax.axis_size(axis))
    arrived = lax.all_to_all(tiles, axis, split_axis=0, concat_axis=0, tiled=True)
    return arrived.sum(axis=0)


def in_one_piece(arrays, axis, dim, along):
    columns = [a.reshape(*a.shape[:along], -1) for a in arrays]
    both = jnp.concatenate(columns, axis=along)
    out, at, finished = (summed_on_arrival(both, axis, dim), 0, [])
    for a, column in zip(arrays, columns):
        slab = out[..., at : at + column.shape[along]]
        finished.append(slab.reshape(*slab.shape[:along], *a.shape[along:]))
        at += column.shape[along]
    return tuple(finished)


def attend(query_rows, keys, lengths, positions):
    draft = query_rows.shape[1]
    scale = (NOPE + ROPE) ** (-0.5)
    scores = (
        jnp.einsum("bdhk,btk->bdht", query_rows, keys, preferred_element_type=jnp.float32) * scale
    )
    limit = lengths[:, None] - draft + jnp.arange(draft, dtype=jnp.int32)[None, :]
    visible = positions[None, None, None, :] <= limit[:, :, None, None]
    masked = jnp.where(visible, scores, jnp.float32(-1e30))
    peak = jnp.max(masked, axis=3)
    weights = jnp.where(visible, jnp.exp(masked - peak[..., None]), jnp.float32(0.0))
    total = jnp.sum(weights, axis=3)
    latent = keys[:, :, :LAT]
    numerator = jnp.einsum(
        "bdht,btl->bdhl", weights.astype(jnp.bfloat16), latent, preferred_element_type=jnp.float32
    )
    return (numerator, peak, total)


def body(queries, cache, lengths):
    tokens_here = cache.shape[1]
    seq_index = lax.axis_index("seq")
    query_rows = collect(queries, "seq", 2)
    positions = seq_index * tokens_here + jnp.arange(tokens_here, dtype=jnp.int32)
    numerator, peak, total = attend(query_rows, cache, lengths, positions)
    highest = of_everyone(peak, "seq")
    factor = jnp.exp(peak - highest)
    numerator, total = in_one_piece((numerator * factor[..., None], total * factor), "seq", 2, 3)
    return (numerator / total[..., None]).astype(jnp.bfloat16)


def solution(mesh):
    return jax.shard_map(
        body,
        mesh=mesh,
        in_specs=(
            P(("group", "batch"), None, ("seq", "head"), None),
            P(("group", "batch"), "seq", None),
            P(("group", "batch")),
        ),
        out_specs=P(("group", "batch"), None, ("seq", "head"), None),
        check_vma=False,
    )
```

profile of v0, /device:TPU:74, one launch (start us, length us, event | category | flops | bytes accessed | tf_op | source)
XLA Modules:
  0.0 181.4 jit_solution(3786255015262253566)
XLA Ops:
  0.0 1.8 broadcast_in_dim.31
  1.8 43.7 %all-to-all-start = ((bf16[16,2,4,4,576]{4,3,2,1,0:T(4,128)(2,1)}), bf16[16,2,4,4,576]{4,3,2,1,0:T(4,128)(2,1)S(1)}, u32[]{:S(2)}, u32[]{:S(2)}) async-start(bf16[16,2,4,4,576]{4,3,2,1,0:T(4,128)(2,1)} %broadcast_in_dim.31), calls=%async_computation | async-start | bytes 1310720 | tf_op jit(solution)/shard_map/all_to_all | solution.py:19
  45.5 0.7 broadcast_add_fusion
  46.2 0.1 iota_add_fusion.1
  46.2 0.1 broadcast_compare_fusion
  46.3 32.8 %all-to-all-done = bf16[16,2,4,4,576]{4,3,2,1,0:T(4,128)(2,1)S(1)} async-done(((bf16[16,2,4,4,576]{4,3,2,1,0:T(4,128)(2,1)}), bf16[16,2,4,4,576]{4,3,2,1,0:T(4,128)(2,1)S(1)}, u32[]{:S(2)}, u32[]{:S(2)}) %all-to-all-start) | async-done | bytes 589856 | tf_op jit(solution)/shard_map/all_to_all | solution.py:19
  79.1 0.2 copy.16
  79.3 0.3 reshape.82
  79.7 6.2 %fusion.5 = (f32[2,4,64]{2,1,0:T(4,128)S(1)}, f32[2,4,64,2048]{3,2,1,0:T(8,128)}) fusion(pred[2,4,2048]{2,1,0:T(4,128)(4,1)S(1)} %broadcast_compare_fusion, bf16[2,4,64,576]{3,2,1,0:T(8,128)(2,1)S(1)} %reshape.82, bf16[2,2048,576]{1,2,0:T(8,128)(2,1)} %param.4), kind=kOutput, calls=%fused_computation.7 | convolution fusion | flops 1211104768 | bytes 9521152 | tf_op jit(solution)/shard_map/bdhk,btk->bdht/dot_general | solution.py:57
  85.9 0.7 reshape.86
  86.6 7.5 %all-to-all-start.1 = ((f32[16,1,512]{2,1,0:T(1,128)}), f32[16,1,512]{2,1,0:T(1,128)S(1)}, u32[]{:S(2)}, u32[]{:S(2)}) async-start(f32[16,1,512]{2,1,0:T(1,128)} %reshape.86), calls=%async_computation.1 | async-start | bytes 65536 | tf_op jit(solution)/shard_map/all_to_all | solution.py:19
  94.1 3.5 %fusion.6 = f32[2,4,64]{2,1,0:T(4,128)S(1)} fusion(f32[2,4,64,2048]{3,2,1,0:T(8,128)} %get-tuple-element.8, f32[2,4,64]{2,1,0:T(4,128)S(1)} %get-tuple-element.7, pred[2,4,2048]{2,1,0:T(4,128)(4,1)S(1)} %broadcast_compare_fusion), kind=kLoop, calls=%fused_computation.8 | loop fusion | flops 5242368 | bytes 4214784 | tf_op jit(solution)/shard_map/reduce_sum | solution.py:64
  97.6 8.9 %all-to-all-done.1 = f32[16,1,512]{2,1,0:T(1,128)S(1)} async-done(((f32[16,1,512]{2,1,0:T(1,128)}), f32[16,1,512]{2,1,0:T(1,128)S(1)}, u32[]{:S(2)}, u32[]{:S(2)}) %all-to-all-start.1) | async-done | bytes 32800 | tf_op jit(solution)/shard_map/all_to_all | solution.py:19
  106.4 0.5 broadcast.39
  106.9 0.7 reduce.2
  107.7 0.1 reshape.87
  107.8 4.8 %fusion.14 = f32[2,4,64,512]{3,2,1,0:T(8,128)S(1)} fusion(bf16[2,2048,576]{1,2,0:T(8,128)(2,1)} %param.4, f32[2,4,64,2048]{3,2,1,0:T(8,128)} %get-tuple-element.8, f32[2,4,64]{2,1,0:T(4,128)S(1)} %get-tuple-element.7, pred[2,4,2048]{2,1,0:T(4,128)(4,1)S(1)} %broadcast_compare_fusion, f32[2,4,64]{2,1,0:T(4,128)S(1)} %bitcast.31), kind=kOutput, calls=%fused_computation.15 | convolution fusion | flops 1079246848 | bytes 9457664 | tf_op jit(solution)/shard_map/bdht,btl->bdhl/dot_general | solution.py:66
  112.6 0.3 concatenate.6
  112.9 0.1 mul.37
  113.0 0.9 copy.20
  113.9 0.3 maximum_bitcast_fusion
  114.3 66.1 %all_to_all.15 = f32[16,2,4,4,513]{4,3,2,1,0:T(4,128)S(1)} all-to-all(f32[16,2,4,4,513]{4,3,2,1,0:T(4,128)S(1)} %maximum_bitcast_fusion), channel_id=1, replica_groups=mesh['group'=2,'seq'=16,'batch'=8,'head'=2] {'seq'}, dimensions={0} | all-to-all | bytes 2101248 | tf_op jit(solution)/shard_map/all_to_all | solution.py:38
  180.4 0.2 reduce_sum.19
  180.6 0.1 slice_reduce_fusion
  180.7 0.7 fusion.19
  (4 shorter events, 0.1 us)
Async XLA Ops:
  1.8 77.3 %all-to-all-start = ((bf16[16,2,4,4,576]{4,3,2,1,0:T(4,128)(2,1)}), bf16[16,2,4,4,576]{4,3,2,1,0:T(4,128)(2,1)S(1)}, u32[]{:S(2)}, u32[]{:S(2)}) async-start(bf16[16,2,4,4,576]{4,3,2,1,0:T(4,128)(2,1)} %broadcast_in_dim.31), calls=%async_computation | async-start | bytes 1310720 | tf_op jit(solution)/shard_map/all_to_all | solution.py:19
  86.6 19.8 %all-to-all-start.1 = ((f32[16,1,512]{2,1,0:T(1,128)}), f32[16,1,512]{2,1,0:T(1,128)S(1)}, u32[]{:S(2)}, u32[]{:S(2)}) async-start(f32[16,1,512]{2,1,0:T(1,128)} %reshape.86), calls=%async_computation.1 | async-start | bytes 65536 | tf_op jit(solution)/shard_map/all_to_all | solution.py:19
where the time goes:
time: 182 us; the launch traced here: 181 us
  blocking collectives  66.1 us (36%)
  starting transfers between devices  51.1 us (28%)
  waiting for transfers between devices  41.6 us (23%)
  matrix products  11 us (6%)
  other arithmetic  6.36 us (3%)
  local copies, waits for them, and re-layouts  5.05 us (3%)
    all_to_all x1, blocking collectives, summed_on_arrival(): lax.all_to_all(tiles, axis, split_axis=0, concat_axis=0, tiled=True)  66.1 us
    all_to_all x2, starting transfers between devices, copy_for_each(): return lax.all_to_all(copies, axis, split_axis=0, concat_axis=0, tiled=True)  51.1 us
    all_to_all x2, waiting for transfers between devices, copy_for_each(): return lax.all_to_all(copies, axis, split_axis=0, concat_axis=0, tiled=True)  41.6 us
    dot_general x1, matrix products, attend(): jnp.einsum('bdhk,btk->bdht', query_rows, keys, preferred_element_type=jnp...  6.2 us
    dot_general x1, matrix products, attend(): jnp.einsum('bdht,btl->bdhl', weights.astype(jnp.bfloat16), latent, prefer...  4.81 us
  transfers between devices with their start and end apart: 2, of which 2 were waited for; matrix products, arithmetic and copies ran while one was open for 2% of the time, Pallas kernels for 0%

commit v1 on v0

v1 whole, which is shorter than its diff:
```python
import functools
import math

import jax
import jax.numpy as jnp
from jax import lax
from jax.experimental import pallas as pl
from jax.experimental.pallas import tpu as pltpu
from jax.sharding import PartitionSpec as P

LAT = 512
ROPE = 64
NOPE = 128
LANES = 128
STAT_ROWS = 8
HIDDEN = -1e30
FLOOR = -1e25


def attend_kernel(chunk, seqs, draft, heads, peers, lengths_ref, first_ref, q_hbm, cache_hbm, out_ref,
                  q_vmem, k_vmem, s_vmem, q_sem, k_sem):
    tokens = cache_hbm.shape[1]
    chunks = tokens // chunk
    own = draft * heads
    rows = peers * own
    q_copy = pltpu.make_async_copy(q_hbm, q_vmem, q_sem)
    q_copy.start()
    copies = {}
    for b in range(seqs):
        for c in range(chunks):
            part = pl.ds(c * chunk, chunk)
            copies[b, c] = pltpu.make_async_copy(cache_hbm.at[b, part], k_vmem.at[b, part], k_sem.at[b, c])
            copies[b, c].start()
    q_copy.wait()
    scale = (NOPE + ROPE) ** (-0.5) * math.log2(math.e)
    row = lax.broadcasted_iota(jnp.int32, (rows, 1), 0)
    member = (row // heads) % draft
    lane = lax.broadcasted_iota(jnp.int32, (rows, LANES), 1)
    stats = jnp.zeros((rows, LANES), jnp.float32)
    first = first_ref[0]
    for b in range(seqs):
        q = q_vmem[:, b].reshape(rows, q_vmem.shape[-1])
        limit = lengths_ref[b] - draft - first + member
        tops = None
        for c in range(chunks):
            copies[b, c].wait()
            keys = k_vmem[b, c * chunk : (c + 1) * chunk]
            s = lax.dot_general(q, keys, (((1,), (1,)), ((), ())), preferred_element_type=jnp.float32)
            at = c * chunk + lax.broadcasted_iota(jnp.int32, (rows, chunk), 1)
            s = jnp.where(at <= limit, s * scale, HIDDEN)
            s_vmem[b, :, c * chunk : (c + 1) * chunk] = s
            for i in range(chunk // LANES):
                tile = s[:, i * LANES : (i + 1) * LANES]
                tops = tile if tops is None else jnp.maximum(tops, tile)
        peak = jnp.maximum(jnp.max(tops, axis=1, keepdims=True), FLOOR)
        point = peak.astype(jnp.bfloat16).astype(jnp.float32)
        sums = jnp.zeros((rows, LANES), jnp.float32)
        numerator = jnp.zeros((rows, LAT), jnp.float32)
        for c in range(chunks):
            w = jnp.exp2(s_vmem[b, :, c * chunk : (c + 1) * chunk] - point)
            for i in range(chunk // LANES):
                sums = sums + w[:, i * LANES : (i + 1) * LANES]
            values = k_vmem[b, c * chunk : (c + 1) * chunk, :LAT]
            numerator = numerator + jnp.dot(w.astype(jnp.bfloat16), values, preferred_element_type=jnp.float32)
        total = jnp.sum(sums, axis=1, keepdims=True)
        inverse = jnp.where(total > 0.0, 1.0 / total, 0.0)
        part = (numerator * inverse).astype(jnp.bfloat16)
        for i in range(LAT // LANES):
            tile = part[:, i * LANES : (i + 1) * LANES].reshape(peers, own, LANES)
            at = (i * seqs + b) * own
            out_ref[:, at : at + own, :] = tile
        high = total.astype(jnp.bfloat16).astype(jnp.float32)
        for i, value in enumerate((point, high, total - high)):
            stats = jnp.where(lane == 4 * b + i, value, stats)
    across = stats.T[:STAT_ROWS]
    base = seqs * own * (LAT // LANES)
    for p in range(peers):
        tile, at = divmod(p * own, LANES)
        mine = across[:, tile * LANES : (tile + 1) * LANES]
        if at:
            mine = pltpu.roll(mine, LANES - at, 1)
        out_ref[p, base : base + STAT_ROWS, :] = mine.astype(jnp.bfloat16)


def combine_kernel(seqs, draft, heads, peers, in_ref, out_ref):
    own = draft * heads
    base = seqs * own * (LAT // LANES)
    for b in range(seqs):
        stat = [in_ref[:, base + 4 * b + i, :].astype(jnp.float32) for i in range(3)]
        point, total = stat[0], stat[1] + stat[2]
        weight = total * jnp.exp2(point - jnp.max(point, axis=0, keepdims=True))
        weight = weight / jnp.sum(weight, axis=0, keepdims=True)
        column = jnp.concatenate([weight, jnp.zeros((LANES - peers, LANES), jnp.float32)], axis=0).T[:own]
        for i in range(LAT // LANES):
            at = (i * seqs + b) * own
            acc = jnp.zeros((own, LANES), jnp.float32)
            for p in range(peers):
                acc = acc + column[:, p : p + 1] * in_ref[p, at : at + own, :].astype(jnp.float32)
            out_ref[b, :, :, i * LANES : (i + 1) * LANES] = (
                acc.reshape(draft, heads, LANES).astype(jnp.bfloat16)
            )


def body(queries, cache, lengths):
    seqs, draft, heads, width = queries.shape
    tokens = cache.shape[1]
    peers = lax.axis_size("seq")
    own = draft * heads
    rows = peers * own
    chunk = 512
    message = seqs * own * (LAT // LANES) + STAT_ROWS
    everyone = lax.all_gather(queries.reshape(seqs, own, width), "seq", axis=0)
    first = (lax.axis_index("seq") * tokens).astype(jnp.int32).reshape(1)
    any_spec = pl.BlockSpec(memory_space=pl.ANY)
    smem = pl.BlockSpec(memory_space=pltpu.SMEM)
    partial = pl.pallas_call(
        functools.partial(attend_kernel, chunk, seqs, draft, heads, peers),
        out_shape=jax.ShapeDtypeStruct((peers, message, LANES), jnp.bfloat16),
        in_specs=[smem, smem, any_spec, any_spec],
        out_specs=pl.BlockSpec(memory_space=pltpu.VMEM),
        scratch_shapes=[
            pltpu.VMEM((peers, seqs, own, width), jnp.bfloat16),
            pltpu.VMEM((seqs, tokens, width), jnp.bfloat16),
            pltpu.VMEM((seqs, rows, tokens), jnp.float32),
            pltpu.SemaphoreType.DMA,
            pltpu.SemaphoreType.DMA((seqs, tokens // chunk)),
        ],
        name="attend",
    )(lengths, first, everyone, cache)
    arrived = lax.all_to_all(partial, "seq", split_axis=0, concat_axis=0, tiled=True)
    return pl.pallas_call(
        functools.partial(combine_kernel, seqs, draft, heads, peers),
        out_shape=jax.ShapeDtypeStruct((seqs, draft, heads, LAT), jnp.bfloat16),
        in_specs=[pl.BlockSpec(memory_space=pltpu.VMEM)],
        out_specs=pl.BlockSpec(memory_space=pltpu.VMEM),
        name="combine",
    )(arrived)


def solution(mesh):
    return jax.shard_map(
        body,
        mesh=mesh,
        in_specs=(
            P(("group", "batch"), None, ("seq", "head"), None),
            P(("group", "batch"), "seq", None),
            P(("group", "batch")),
        ),
        out_specs=P(("group", "batch"), None, ("seq", "head"), None),
        check_vma=False,
    )
```

time: 182 us -> 126 us (0.69)
  the two profiles are of different devices: /device:TPU:74 before, /device:TPU:84 now
where the time goes in v1:
time: 126 us
  blocking collectives  106 us (84%)
  Pallas kernels  11.1 us (9%)
  local copies, waits for them, and re-layouts  8.5 us (7%)
    all_gather x1, blocking collectives, body(): everyone = lax.all_gather(queries.reshape(seqs, own, width), 'seq', axis=0)  74.1 us
    all_to_all x1, blocking collectives, body(): lax.all_to_all(partial, 'seq', split_axis=0, concat_axis=0, tiled=True)  32 us
    pallas_call x1, Pallas kernels, body(): pl.pallas_call(functools.partial(attend_kernel, chunk, seqs, draft, heads...  9.12 us
    unnamed x1, local copies, waits for them, and re-layouts  7.7 us

profile of v1, /device:TPU:84, one launch (start us, length us, event | category | flops | bytes accessed | tf_op | source)
XLA Modules:
  0.0 125.8 jit_solution(1700500594650292005)
XLA Ops:
  0.0 0.8 all_gather_reshape.3
  0.8 74.1 %all_gather.3.q_hbm = bf16[16,2,16,576]{3,2,1,0:T(8,128)(2,1)} all-gather(bf16[1,2,16,576]{3,2,1,0:T(8,128)(2,1)S(1)} %all_gather_reshape.3), channel_id=1, replica_groups=mesh['group'=2,'seq'=16,'batch'=8,'head'=2] {'seq'}, dimensions={0}, use_global_device_ids=true | all-gather | bytes 626688 | tf_op jit(solution)/shard_map/all_gather | solution.py:112
  74.9 7.7 %copy.5.cache_hbm = bf16[2,2048,576]{2,1,0:T(8,128)(2,1)} copy(bf16[2,2048,576]{1,2,0:T(8,128)(2,1)} %param.4) | data formatting | bytes 9437184 | tf_op args[1]
  82.6 9.1 %attend.1 = bf16[16,136,128]{2,1,0:T(8,128)(2,1)} custom-call(s32[2]{0:T(128)} %lengths_ref.1, s32[1]{0:T(128)} %bitcast.first_ref, bf16[16,2,16,576]{3,2,1,0:T(8,128)(2,1)} %all_gather.3.q_hbm, bf16[2,2048,576]{2,1,0:T(8,128)(2,1)} %copy.5.cache_hbm), custom_call_target="tpu_custom_call" | custom-call | tf_op jit(solution)/shard_map/attend/pallas_call | solution.py:116
  91.7 32.0 %all_to_all.5.in_ref = bf16[16,136,128]{2,1,0:T(8,128)(2,1)} all-to-all(bf16[16,136,128]{2,1,0:T(8,128)(2,1)} %attend.1), channel_id=1, replica_groups=mesh['group'=2,'seq'=16,'batch'=8,'head'=2] {'seq'}, dimensions={0} | all-to-all | bytes 1114112 | tf_op jit(solution)/shard_map/all_to_all | solution.py:130
  123.8 2.0 %combine.1 = bf16[2,4,4,512]{3,2,1,0:T(4,128)(2,1)} custom-call(bf16[16,136,128]{2,1,0:T(8,128)(2,1)} %all_to_all.5.in_ref), custom_call_target="tpu_custom_call" | custom-call | tf_op jit(solution)/shard_map/combine/pallas_call | solution.py:131

commit v2 on v1

v2 whole, which is shorter than its diff:
```python
import functools
import math

import jax
import jax.numpy as jnp
from jax import lax
from jax.experimental import pallas as pl
from jax.experimental.pallas import tpu as pltpu
from jax.sharding import PartitionSpec as P

LAT = 512
ROPE = 64
NOPE = 128
LANES = 128
STAT_ROWS = 8
HIDDEN = -1e30
FLOOR = -1e25


def pack_kernel(seqs, q_ref, out_ref):
    own = q_ref.shape[1] * q_ref.shape[2]
    for b in range(seqs):
        q = q_ref[b].reshape(own, q_ref.shape[-1])
        for i in range(LAT // LANES):
            at = (i * seqs + b) * own
            out_ref[at : at + own, :] = q[:, i * LANES : (i + 1) * LANES]
        out_ref[LAT // LANES * seqs * own :, b * ROPE : (b + 1) * ROPE] = q[:, LAT:]


def attend_kernel(chunk, seqs, draft, heads, order, lengths_ref, q_ref, k_ref, out_ref, s_vmem):
    tokens = k_ref.shape[2]
    chunks = tokens // chunk
    own = draft * heads
    peers = len(order)
    rows = peers * own
    tiles = LAT // LANES
    scale = (NOPE + ROPE) ** (-0.5) * math.log2(math.e)
    row = lax.broadcasted_iota(jnp.int32, (rows, 1), 0)
    member = (row // heads) % draft
    lane = lax.broadcasted_iota(jnp.int32, (rows, LANES), 1)
    stats = jnp.zeros((rows, LANES), jnp.float32)
    for b in range(seqs):
        pieces = [
            q_ref[:, (i * seqs + b) * own : (i * seqs + b + 1) * own, :].reshape(rows, LANES) for i in range(tiles)
        ]
        rotary = q_ref[:, tiles * seqs * own :, :].reshape(rows, LANES)
        q = jnp.concatenate(pieces + [rotary[:, b * ROPE : (b + 1) * ROPE]], axis=1)
        limit = lengths_ref[b] - draft - lax.axis_index("seq") * tokens + member
        tops = None
        for c in range(chunks):
            keys = k_ref[b, :, c * chunk : (c + 1) * chunk]
            s = jnp.dot(q, keys, preferred_element_type=jnp.float32)
            at = c * chunk + lax.broadcasted_iota(jnp.int32, (rows, chunk), 1)
            s = jnp.where(at <= limit, s * scale, HIDDEN)
            s_vmem[b, :, c * chunk : (c + 1) * chunk] = s
            for i in range(chunk // LANES):
                tile = s[:, i * LANES : (i + 1) * LANES]
                tops = tile if tops is None else jnp.maximum(tops, tile)
        peak = jnp.maximum(jnp.max(tops, axis=1, keepdims=True), FLOOR)
        point = peak.astype(jnp.bfloat16).astype(jnp.float32)
        sums = jnp.zeros((rows, LANES), jnp.float32)
        numerator = jnp.zeros((rows, LAT), jnp.float32)
        for c in range(chunks):
            w = jnp.exp2(s_vmem[b, :, c * chunk : (c + 1) * chunk] - point)
            for i in range(chunk // LANES):
                sums = sums + w[:, i * LANES : (i + 1) * LANES]
            values = k_ref[b, :LAT, c * chunk : (c + 1) * chunk]
            numerator = numerator + lax.dot_general(
                w.astype(jnp.bfloat16), values, (((1,), (1,)), ((), ())), preferred_element_type=jnp.float32
            )
        total = jnp.sum(sums, axis=1, keepdims=True)
        inverse = jnp.where(total > 0.0, 1.0 / total, 0.0)
        part = (numerator * inverse).astype(jnp.bfloat16)
        for i in range(tiles):
            at = (i * seqs + b) * own
            for slot, p in enumerate(order):
                out_ref[p, at : at + own, :] = part[slot * own : (slot + 1) * own, i * LANES : (i + 1) * LANES]
        high = total.astype(jnp.bfloat16).astype(jnp.float32)
        for i, value in enumerate((point, high, total - high)):
            stats = jnp.where(lane == 4 * b + i, value, stats)
    across = stats.T[:STAT_ROWS]
    base = seqs * own * tiles
    for slot, p in enumerate(order):
        tile, at = divmod(slot * own, LANES)
        mine = across[:, tile * LANES : (tile + 1) * LANES]
        if at:
            mine = pltpu.roll(mine, LANES - at, 1)
        out_ref[p, base : base + STAT_ROWS, :] = mine.astype(jnp.bfloat16)


def combine_kernel(seqs, draft, heads, peers, in_ref, out_ref):
    own = draft * heads
    base = seqs * own * (LAT // LANES)
    for b in range(seqs):
        stat = [in_ref[:, base + 4 * b + i, :].astype(jnp.float32) for i in range(3)]
        point, total = stat[0], stat[1] + stat[2]
        weight = total * jnp.exp2(point - jnp.max(point, axis=0, keepdims=True))
        weight = weight / jnp.sum(weight, axis=0, keepdims=True)
        column = jnp.concatenate([weight, jnp.zeros((LANES - peers, LANES), jnp.float32)], axis=0).T[:own]
        for i in range(LAT // LANES):
            at = (i * seqs + b) * own
            acc = jnp.zeros((own, LANES), jnp.float32)
            for p in range(peers):
                acc = acc + column[:, p : p + 1] * in_ref[p, at : at + own, :].astype(jnp.float32)
            out_ref[b, :, :, i * LANES : (i + 1) * LANES] = (
                acc.reshape(draft, heads, LANES).astype(jnp.bfloat16)
            )


def body(queries, cache, lengths):
    seqs, draft, heads, width = queries.shape
    tokens = cache.shape[1]
    peers = lax.axis_size("seq")
    own = draft * heads
    rows = peers * own
    chunk = 512
    packed = seqs * own * width // LANES
    message = seqs * own * (LAT // LANES) + STAT_ROWS
    vmem = pl.BlockSpec(memory_space=pltpu.VMEM)
    smem = pl.BlockSpec(memory_space=pltpu.SMEM)
    mine = pl.pallas_call(
        functools.partial(pack_kernel, seqs),
        out_shape=jax.ShapeDtypeStruct((packed, LANES), jnp.bfloat16),
        in_specs=[vmem],
        out_specs=vmem,
        cost_estimate=pl.CostEstimate(flops=5_000_000_000, bytes_accessed=150_000, transcendentals=0),
        compiler_params=pltpu.CompilerParams(vmem_limit_bytes=4 * 1024 * 1024),
        name="pack",
    )(queries)
    everyone = lax.all_gather(mine, "seq", axis=0)
    partial = pl.pallas_call(
        functools.partial(attend_kernel, chunk, seqs, draft, heads, list(range(peers))),
        out_shape=jax.ShapeDtypeStruct((peers, message, LANES), jnp.bfloat16),
        in_specs=[smem, vmem, vmem],
        out_specs=vmem,
        scratch_shapes=[pltpu.VMEM((seqs, rows, tokens), jnp.float32)],
        compiler_params=pltpu.CompilerParams(vmem_limit_bytes=24 * 1024 * 1024),
        name="attend",
    )(lengths, everyone, jnp.swapaxes(cache, 1, 2))
    arrived = lax.all_to_all(partial, "seq", split_axis=0, concat_axis=0, tiled=True)
    return pl.pallas_call(
        functools.partial(combine_kernel, seqs, draft, heads, peers),
        out_shape=jax.ShapeDtypeStruct((seqs, draft, heads, LAT), jnp.bfloat16),
        in_specs=[vmem],
        out_specs=vmem,
        compiler_params=pltpu.CompilerParams(vmem_limit_bytes=8 * 1024 * 1024),
        name="combine",
    )(arrived)


def solution(mesh):
    return jax.shard_map(
        body,
        mesh=mesh,
        in_specs=(
            P(("group", "batch"), None, ("seq", "head"), None),
            P(("group", "batch"), "seq", None),
            P(("group", "batch")),
        ),
        out_specs=P(("group", "batch"), None, ("seq", "head"), None),
        check_vma=False,
    )
```

time: 126 us -> 109 us (0.87)
  the two profiles are of different devices: /device:TPU:84 before, /device:TPU:88 now
where the time goes in v2:
time: 109 us
  blocking collectives  102 us (94%)
  Pallas kernels  5.38 us (5%)
    all_gather x1, blocking collectives, body(): everyone = lax.all_gather(mine, 'seq', axis=0)  71.4 us
    all_to_all x1, blocking collectives, body(): lax.all_to_all(partial, 'seq', split_axis=0, concat_axis=0, tiled=True)  31 us
    pallas_call x1, Pallas kernels, body(): pl.pallas_call(functools.partial(attend_kernel, chunk, seqs, draft, heads...  4.37 us

profile of v2, /device:TPU:88, one launch (start us, length us, event | category | flops | bytes accessed | tf_op | source)
XLA Modules:
  0.0 108.6 jit_solution(6431735097834153731)
XLA Ops:
  0.0 0.0 copy-start.1
  0.0 0.0 copy-start.2
  0.0 0.8 copy-done.2
  0.8 0.0 copy-start
  0.8 0.1 pack.1
  0.9 71.4 %all-gather = bf16[2304,128]{1,0:T(8,128)(2,1)S(1)} all-gather(bf16[144,128]{1,0:T(8,128)(2,1)S(1)} %pack.1), channel_id=2, replica_groups=mesh['group'=2,'seq'=16,'batch'=8,'head'=2] {'seq'}, dimensions={0}, use_global_device_ids=true | all-gather | bytes 626688 | tf_op jit(solution)/shard_map/all_gather | solution.py:130
  72.3 0.0 copy-done.1
  72.3 0.0 copy-done
  72.3 4.4 %attend.1 = bf16[16,136,128]{2,1,0:T(8,128)(2,1)S(1)} custom-call(s32[2]{0:T(128)S(1)} %copy-done.1, bf16[16,144,128]{2,1,0:T(8,128)(2,1)S(1)} %bitcast.3, bf16[2,576,2048]{2,1,0:T(8,128)(2,1)S(1)} %bitcast.2), custom_call_target="tpu_custom_call" | custom-call | tf_op jit(solution)/shard_map/attend/pallas_call | solution.py:131
  76.7 31.0 %all_to_all.5.in_ref = bf16[16,136,128]{2,1,0:T(8,128)(2,1)S(1)} all-to-all(bf16[16,136,128]{2,1,0:T(8,128)(2,1)S(1)} %attend.1), channel_id=1, replica_groups=mesh['group'=2,'seq'=16,'batch'=8,'head'=2] {'seq'}, dimensions={0} | all-to-all | bytes 1114112 | tf_op jit(solution)/shard_map/all_to_all | solution.py:140
  107.7 0.9 combine.1
Async XLA Ops:
  0.0 72.3 %copy-start.1 = (s32[2]{0:T(128)S(1)}, s32[2]{0:T(128)}, u32[]{:S(2)}) copy-start(s32[2]{0:T(128)} %lengths_ref.1) | copy-start | bytes 28
  0.0 0.8 copy-start.2
  0.8 71.5 %copy-start = (bf16[2,2048,576]{1,2,0:T(8,128)(2,1)S(1)}, bf16[2,2048,576]{1,2,0:T(8,128)(2,1)}, u32[]{:S(2)}) copy-start(bf16[2,2048,576]{1,2,0:T(8,128)(2,1)} %param.4) | copy-start | bytes 14155780

commit v3 on v2

--- a/solution.py
+++ b/solution.py
@@ -39,6 +39,7 @@
     member = (row // heads) % draft
     lane = lax.broadcasted_iota(jnp.int32, (rows, LANES), 1)
     stats = jnp.zeros((rows, LANES), jnp.float32)
+    highs = []
     for b in range(seqs):
         pieces = [
             q_ref[:, (i * seqs + b) * own : (i * seqs + b + 1) * own, :].reshape(rows, LANES) for i in range(tiles)
@@ -56,7 +57,9 @@
             for i in range(chunk // LANES):
                 tile = s[:, i * LANES : (i + 1) * LANES]
                 tops = tile if tops is None else jnp.maximum(tops, tile)
-        peak = jnp.maximum(jnp.max(tops, axis=1, keepdims=True), FLOOR)
+        highs.append(tops)
+    for b in range(seqs):
+        peak = jnp.maximum(jnp.max(highs[b], axis=1, keepdims=True), FLOOR)
         point = peak.astype(jnp.bfloat16).astype(jnp.float32)
         sums = jnp.zeros((rows, LANES), jnp.float32)
         numerator = jnp.zeros((rows, LAT), jnp.float32)
@@ -113,7 +116,7 @@
     peers = lax.axis_size("seq")
     own = draft * heads
     rows = peers * own
-    chunk = 512
+    chunk = 1024
     packed = seqs * own * width // LANES
     message = seqs * own * (LAT // LANES) + STAT_ROWS
     vmem = pl.BlockSpec(memory_space=pltpu.VMEM)

time: 109 us -> 108 us (level)
  the two profiles are of different devices: /device:TPU:88 before, /device:TPU:86 now
where the time goes in v3:
time: 108 us
  blocking collectives  102 us (94%)
  Pallas kernels  5.06 us (5%)
    all_gather x1, blocking collectives, body(): everyone = lax.all_gather(mine, 'seq', axis=0)  71.4 us
    all_to_all x1, blocking collectives, body(): lax.all_to_all(partial, 'seq', split_axis=0, concat_axis=0, tiled=True)  31 us
    pallas_call x1, Pallas kernels, body(): pl.pallas_call(functools.partial(attend_kernel, chunk, seqs, draft, heads...  4.06 us

profile of v3, /device:TPU:86, one launch (start us, length us, event | category | flops | bytes accessed | tf_op | source)
XLA Modules:
  0.0 108.3 jit_solution(10365040696695844664)
XLA Ops:
  0.0 0.0 copy-start.1
  0.0 0.0 copy-start.2
  0.0 0.8 copy-done.2
  0.8 0.0 copy-start
  0.8 0.1 pack.1
  0.9 71.4 %all-gather = bf16[2304,128]{1,0:T(8,128)(2,1)S(1)} all-gather(bf16[144,128]{1,0:T(8,128)(2,1)S(1)} %pack.1), channel_id=2, replica_groups=mesh['group'=2,'seq'=16,'batch'=8,'head'=2] {'seq'}, dimensions={0}, use_global_device_ids=true | all-gather | bytes 626688 | tf_op jit(solution)/shard_map/all_gather | solution.py:133
  72.3 0.0 copy-done.1
  72.3 0.0 copy-done
  72.3 4.1 %attend.1 = bf16[16,136,128]{2,1,0:T(8,128)(2,1)S(1)} custom-call(s32[2]{0:T(128)S(1)} %copy-done.1, bf16[16,144,128]{2,1,0:T(8,128)(2,1)S(1)} %bitcast.3, bf16[2,576,2048]{2,1,0:T(8,128)(2,1)S(1)} %bitcast.2), custom_call_target="tpu_custom_call" | custom-call | tf_op jit(solution)/shard_map/attend/pallas_call | solution.py:134
  76.4 31.0 %all_to_all.5.in_ref = bf16[16,136,128]{2,1,0:T(8,128)(2,1)S(1)} all-to-all(bf16[16,136,128]{2,1,0:T(8,128)(2,1)S(1)} %attend.1), channel_id=1, replica_groups=mesh['group'=2,'seq'=16,'batch'=8,'head'=2] {'seq'}, dimensions={0} | all-to-all | bytes 1114112 | tf_op jit(solution)/shard_map/all_to_all | solution.py:143
  107.4 0.9 combine.1
Async XLA Ops:
  0.0 72.3 %copy-start.1 = (s32[2]{0:T(128)S(1)}, s32[2]{0:T(128)}, u32[]{:S(2)}) copy-start(s32[2]{0:T(128)} %lengths_ref.1) | copy-start | bytes 28
  0.0 0.8 copy-start.2
  0.8 71.5 %copy-start = (bf16[2,2048,576]{1,2,0:T(8,128)(2,1)S(1)}, bf16[2,2048,576]{1,2,0:T(8,128)(2,1)}, u32[]{:S(2)}) copy-start(bf16[2,2048,576]{1,2,0:T(8,128)(2,1)} %param.4) | copy-start | bytes 14155780
